TPU v7x, 32 devices: a whole 2x2x4 slice. The times are simulated.
32 devices in a mesh: aa: 8 (over z, x), ba: 4 (over y, core).
Axes of the slice: x: 2, y: 2, z: 4, core: 2. Of those that a mesh axis runs over, the one named last changes fastest.
Arguments:
- residual_a: bfloat16 [64, 4096], P('ba', 'aa'), may hold values from -160 to 160
- residual_b: bfloat16 [64, 3584], P(('aa', 'ba')), may hold values from -160 to 160
- encoder_a: bfloat16 [4096, 16384], P('ba', 'aa'), may hold values from -1 to 1
- bias_a: float32 [16384], P('aa'), may hold values from -12 to 12
- encoder_b: bfloat16 [3584, 16384], P('aa', 'ba'), may hold values from -1 to 1
- bias_b: float32 [16384], P('ba'), may hold values from -12 to 12
Outputs:
- match_score: float32 [16384, 16384], P('aa', 'ba')
- row_level: float32 [16384], P('aa')
- column_level: float32 [16384], P('ba')
All inputs are finite; a program needn't handle non-finite values.
Results may differ from a plain program's by a relative error of at most 0.0004.
The roundings to bfloat16 on the way count: a program that leaves them out, or rounds other values in their place, can miss the bound.
Values may be sent and summed in bfloat16 or wider, within the bound.
No kernel may reach another device: no remote copies, remote signals or barrier semaphores. Data moves between devices by JAX's collectives and lax.ppermute only.
A program may use at most 128 MiB of HBM per device.

v0:
```python
import jax
import jax.numpy as jnp
from jax import lax
from jax.sharding import PartitionSpec as P

INV_TEMP = 256
epsilon = 1e-05


def per_device(residual_a, residual_b, encoder_a, bias_a, encoder_b, bias_b):
    rows_a = lax.all_gather(residual_a, "aa", axis=1, tiled=True)
    inputs = rows_a
    encoded_a = jnp.dot(
        inputs,
        lax.all_gather(encoder_a, "ba", axis=0, tiled=True),
        preferred_element_type=jnp.float32,
    )
    fired_a = jnp.maximum(encoded_a + bias_a[None, :], 0.0)
    rows_b = lax.all_gather(residual_b, "ba", axis=0, tiled=True)
    columns_b = lax.all_to_all(rows_b, "aa", split_axis=1, concat_axis=0, tiled=True)
    inputs = columns_b
    encoded_b = lax.psum_scatter(
        jnp.dot(inputs, encoder_b, preferred_element_type=jnp.float32),
        "aa",
        scatter_dimension=0,
        tiled=True,
    )
    fired_b = jnp.maximum(encoded_b + bias_b[None, :], 0.0)
    token_total = float(rows_a.shape[0] * lax.axis_size("ba"))
    mean_a = lax.psum(jnp.sum(fired_a, 0), "ba") / token_total
    mean_b = lax.psum(jnp.sum(fired_b, 0), "aa") / token_total
    centered_a = fired_a - mean_a[None, :]
    centered_b = fired_b - mean_b[None, :]
    spread_a = lax.psum(jnp.sum(centered_a * centered_a, 0), "ba") / token_total
    spread_b = lax.psum(jnp.sum(centered_b * centered_b, 0), "aa") / token_total
    unit_a = (centered_a * lax.rsqrt(spread_a + epsilon)[None, :]).astype(jnp.bfloat16)
    unit_b = (centered_b * lax.rsqrt(spread_b + epsilon)[None, :]).astype(jnp.bfloat16)
    every_a = lax.all_gather(unit_a, "ba", axis=0, tiled=True)
    correlation = (
        lax.dot_general(
            every_a,
            lax.all_gather(unit_b, "aa", axis=0, tiled=True),
            (((0,), (0,)), ((), ())),
            preferred_element_type=jnp.float32,
        )
        / token_total
    )
    scores = correlation * INV_TEMP
    row_local = jnp.max(scores, axis=1)
    column_local = jnp.max(scores, axis=0)
    row_top = lax.pmax(row_local, "ba")
    column_top = lax.pmax(column_local, "aa")
    row_mass = lax.psum(jnp.sum(jnp.exp(scores - row_top[:, None]), axis=1), "ba")
    column_mass = lax.psum(jnp.sum(jnp.exp(scores - column_top[None, :]), axis=0), "aa")
    row_level = (row_top + jnp.log(row_mass)) / INV_TEMP
    column_level = (column_top + jnp.log(column_mass)) / INV_TEMP
    match_score = correlation - 0.5 * (row_level[:, None] + column_level[None, :])
    return (match_score, row_level, column_level)


def solution(mesh):
    return jax.shard_map(
        per_device,
        mesh=mesh,
        in_specs=(
            P("ba", "aa"),
            P(("aa", "ba"), None),
            P("ba", "aa"),
            P("aa"),
            P("aa", "ba"),
            P("ba"),
        ),
        out_specs=(P("aa", "ba"), P("aa"), P("ba")),
        check_vma=False,
    )
```

profile of v0, /device:TPU:0, one launch (start us, length us, event | category | flops | bytes accessed | tf_op | source)
XLA Modules:
  0.0 375.0 jit_solution(1914857120567517789)
XLA Ops:
  8.0 0.0 reduce-scatter.2.cloned.1.call-start
  8.0 6.5 %all-gather = bf16[4,2,3584]{2,1,0:T(2,128)(2,1)S(1)} all-gather(bf16[1,2,3584]{2,1,0:T(2,128)(2,1)} %bitcast.11), channel_id=1, replica_groups=mesh['aa'=8,'ba'=4] {'ba'}, dimensions={0}, use_global_device_ids=true | all-gather | bytes 71680 | tf_op jit(solution)/shard_map/all_gather | solution.py:19
  14.5 0.1 all_to_all.14
  14.7 12.9 %all_to_all.19 = bf16[8,8,448]{2,0,1:T(8,128)(2,1)S(1)} all-to-all(bf16[8,8,448]{2,0,1:T(8,128)(2,1)S(1)} %copy.10), channel_id=1, replica_groups=mesh['aa'=8,'ba'=4] {'aa'}, dimensions={1} | all-to-all | bytes 114688 | tf_op jit(solution)/shard_map/all_to_all | solution.py:20
  27.6 3.8 %fusion.2 = f32[64,4096]{1,0:T(8,128)} fusion(bf16[448,4096]{1,0:T(8,128)(2,1)} %param.10, bf16[8,8,448]{2,0,1:T(8,128)(2,1)S(1)} %all_to_all.19), kind=kOutput, calls=%fused_computation.13 | convolution fusion | flops 234881024 | bytes 4775936 | tf_op jit(solution)/shard_map/dot_general | solution.py:23
  31.4 0.0 reduce-scatter.2.cloned.1.call-update
  31.4 0.0 all-gather.3.cloned.1.call-start
  31.5 0.5 all-gather.3.cloned.1.call-update
  32.0 30.8 %all_gather.15 = bf16[16,4096]{1,0:T(8,128)(2,1)S(1)} all-gather(bf16[16,512]{1,0:T(8,128)(2,1)} %param.6), channel_id=1, replica_groups=mesh['aa'=8,'ba'=4] {'aa'}, dimensions={1}, use_global_device_ids=true | all-gather | bytes 147456 | tf_op jit(solution)/shard_map/all_gather | solution.py:11
  62.8 30.5 %reduce-scatter.2.cloned.1.call-done = f32[8,4096]{1,0:T(8,128)} async-done(((f32[64,4096]{1,0:T(8,128)}), f32[8,4096]{1,0:T(8,128)}) %reduce-scatter.2.cloned.1.call-update) | async-done | bytes 131088 | tf_op jit(solution)/shard_map/reduce_scatter | solution.py:22
  93.3 1.0 fusion.1
  94.3 35.0 %psum.44 = f32[4096]{0:T(1024)S(1)} all-reduce(f32[4096]{0:T(1024)S(1)} %fusion.1), channel_id=1, replica_groups=mesh['aa'=8,'ba'=4] {'aa'}, use_global_device_ids=true, to_apply=%region_6.0 | all-reduce | flops 4096 | bytes 32768 | tf_op jit(solution)/shard_map/psum | solution.py:31
  129.3 1.0 multiply_reduce_fusion.2
  130.3 33.0 %psum.45 = f32[4096]{0:T(1024)S(1)} all-reduce(f32[4096]{0:T(1024)S(1)} %multiply_reduce_fusion.2), channel_id=1, replica_groups=mesh['aa'=8,'ba'=4] {'aa'}, use_global_device_ids=true, to_apply=%region_8.0 | all-reduce | flops 4096 | bytes 32768 | tf_op jit(solution)/shard_map/psum | solution.py:35
  163.3 0.9 multiply_convert_fusion
  164.2 31.3 %all_gather.19 = bf16[64,4096]{1,0:T(8,128)(2,1)S(1)} all-gather(bf16[8,4096]{1,0:T(8,128)(2,1)S(1)} %multiply_convert_fusion), channel_id=1, replica_groups=mesh['aa'=8,'ba'=4] {'aa'}, dimensions={0}, use_global_device_ids=true | all-gather | bytes 589824 | tf_op jit(solution)/shard_map/all_gather | solution.py:42
  195.5 0.0 all-gather.3.cloned.1.call-done
  195.5 8.1 %fusion.4 = (f32[2048]{0:T(1024)S(1)}, f32[16,2048]{1,0:T(8,128)S(1)}) fusion(f32[2048]{0:T(1024)} %param.9, bf16[16,4096]{1,0:T(8,128)(2,1)S(1)} %all_gather.15, bf16[4096,2048]{1,0:T(8,128)(2,1)} %all-gather.3.cloned.1.call-done), kind=kOutput, calls=%fused_computation.21 | convolution fusion | flops 268531712 | bytes 17055744 | tf_op jit(solution)/shard_map/dot_general | solution.py:13
  203.6 5.8 %psum.42 = f32[2048]{0:T(1024)S(1)} all-reduce(f32[2048]{0:T(1024)S(1)} %get-tuple-element.5), channel_id=1, replica_groups=mesh['aa'=8,'ba'=4] {'ba'}, use_global_device_ids=true, to_apply=%region_1.0 | all-reduce | flops 2048 | bytes 16384 | tf_op jit(solution)/shard_map/psum | solution.py:30
  209.4 6.7 %psum.43 = f32[2048]{0:T(1024)S(1)} all-reduce(f32[2048]{0:T(1024)S(1)} %multiply_reduce_fusion.3), channel_id=1, replica_groups=mesh['aa'=8,'ba'=4] {'ba'}, use_global_device_ids=true, to_apply=%region_3.0 | all-reduce | flops 2048 | bytes 16384 | tf_op jit(solution)/shard_map/psum | solution.py:34
  216.1 5.8 %all_gather.17 = bf16[64,2048]{1,0:T(8,128)(2,1)S(1)} all-gather(bf16[16,2048]{1,0:T(8,128)(2,1)S(1)} %multiply_convert_fusion.1), channel_id=1, replica_groups=mesh['aa'=8,'ba'=4] {'ba'}, dimensions={0}, use_global_device_ids=true | all-gather | bytes 327680 | tf_op jit(solution)/shard_map/all_gather | solution.py:38
  221.9 14.1 %multiply_reduce_fusion.1 = (f32[2048]{0:T(1024)S(1)}, f32[2048,4096]{1,0:T(8,128)}) fusion(bf16[64,2048]{1,0:T(8,128)(2,1)S(1)} %all_gather.17, bf16[64,4096]{1,0:T(8,128)(2,1)S(1)} %all_gather.19), kind=kOutput, calls=%fused_computation.4 | convolution fusion | flops 1090516992 | bytes 34349056 | tf_op jit(solution)/shard_map/dot_general | solution.py:40
  235.9 6.7 %pmax.14 = f32[2048]{0:T(1024)S(1)} all-reduce(f32[2048]{0:T(1024)S(1)} %get-tuple-element.7), channel_id=1, replica_groups=mesh['aa'=8,'ba'=4] {'ba'}, use_global_device_ids=true, to_apply=%region_10.0 | all-reduce | flops 2048 | bytes 16384 | tf_op jit(solution)/shard_map/pmax | solution.py:51
  242.6 15.1 %exponential_reduce_fusion.1 = (f32[2048]{0:T(1024)S(1)}, f32[4096]{0:T(1024)S(1)}) fusion(f32[2048,4096]{1,0:T(8,128)} %get-tuple-element.8, f32[2048]{0:T(1024)S(1)} %pmax.14), kind=kLoop, calls=%fused_computation.2 | loop fusion | flops 33548288 | bytes 33587200 | tf_op jit(solution)/shard_map/reduce_sum | solution.py:53
  257.8 5.8 %psum.46 = f32[2048]{0:T(1024)S(1)} all-reduce(f32[2048]{0:T(1024)S(1)} %get-tuple-element.3), channel_id=1, replica_groups=mesh['aa'=8,'ba'=4] {'ba'}, use_global_device_ids=true, to_apply=%region_12.0 | all-reduce | flops 2048 | bytes 16384 | tf_op jit(solution)/shard_map/psum | solution.py:53
  263.5 0.0 copy-start.1
  263.6 33.0 %pmax.15 = f32[4096]{0:T(1024)S(1)} all-reduce(f32[4096]{0:T(1024)S(1)} %get-tuple-element.4), channel_id=1, replica_groups=mesh['aa'=8,'ba'=4] {'aa'}, use_global_device_ids=true, to_apply=%region_14.0 | all-reduce | flops 4096 | bytes 32768 | tf_op jit(solution)/shard_map/pmax | solution.py:52
  296.5 13.7 %exponential_reduce_fusion = f32[4096]{0:T(1024)S(1)} fusion(f32[2048,4096]{1,0:T(8,128)} %get-tuple-element.8, f32[4096]{0:T(1024)S(1)} %pmax.15), kind=kLoop, calls=%fused_computation.1 | loop fusion | flops 25161728 | bytes 33587200 | tf_op jit(solution)/shard_map/reduce_sum | solution.py:54
  310.3 33.0 %psum.47 = f32[4096]{0:T(1024)S(1)} all-reduce(f32[4096]{0:T(1024)S(1)} %exponential_reduce_fusion), channel_id=1, replica_groups=mesh['aa'=8,'ba'=4] {'aa'}, use_global_device_ids=true, to_apply=%region_16.0 | all-reduce | flops 4096 | bytes 32768 | tf_op jit(solution)/shard_map/psum | solution.py:54
  343.3 0.0 copy-start
  343.3 24.3 %multiply_subtract_fusion = f32[2048,4096]{1,0:T(8,128)} fusion(f32[2048,4096]{1,0:T(8,128)} %get-tuple-element.8, f32[4096]{0:T(1024)S(1)} %add_multiply_fusion, f32[2048]{0:T(1024)S(1)} %add_multiply_fusion.1), kind=kLoop, calls=%fused_computation | loop fusion | flops 33554432 | bytes 67133440 | tf_op jit(solution)/shard_map/sub | solution.py:57
  367.5 0.0 copy-done.1
  367.6 0.0 copy-done
  (9 shorter events, 0.1 us)
Async XLA Ops:
  8.0 85.3 %reduce-scatter.2.cloned.1.call-start = ((), (), s32[]{:S(2)}) async-start(), calls=%async_computation.3 | async-start | bytes 1179648 | tf_op jit(solution)/shard_map/reduce_scatter | solution.py:22
  31.4 164.1 %all-gather.3.cloned.1.call-start = ((), (), s32[]{:S(2)}) async-start(), calls=%async_computation.2 | async-start | bytes 20971520 | tf_op jit(solution)/shard_map/all_gather | solution.py:15
  263.5 104.0 %copy-start.1 = (f32[2048]{0:T(1024)}, f32[2048]{0:T(1024)S(1)}, u32[]{:S(2)}) copy-start(f32[2048]{0:T(1024)S(1)} %add_multiply_fusion.1) | copy-start | bytes 24580
  343.3 24.3 %copy-start = (f32[4096]{0:T(1024)}, f32[4096]{0:T(1024)S(1)}, u32[]{:S(2)}) copy-start(f32[4096]{0:T(1024)S(1)} %add_multiply_fusion) | copy-start | bytes 49156
Sparse Core Ops, SparseCore 0:
  31.5 61.7 reduce-scatter.1
Sparse Core Ops, SparseCore 1:
  33.5 103.3 all-gather.2
where the time goes:
time: 376 us; the launch traced here: 375 us
  blocking collectives  246 us (65%)
  other arithmetic  56.1 us (15%)
  waiting for transfers between devices  31.1 us (8%)
  matrix products  25.9 us (7%)
  between operations  15.6 us (4%)
    psum x1, blocking collectives, per_device(): mean_b = lax.psum(jnp.sum(fired_b, 0), 'aa') / token_total  35 us
    psum x1, blocking collectives, per_device(): spread_b = lax.psum(jnp.sum(centered_b * centered_b, 0), 'aa') / token_total  33 us
    pmax x1, blocking collectives, per_device(): column_top = lax.pmax(column_local, 'aa')  33 us
    psum x1, blocking collectives, per_device(): lax.psum(jnp.sum(jnp.exp(scores - column_top[None, :]), axis=0), 'aa')  33 us
    all_gather x1, blocking collectives, per_device(): lax.all_gather(unit_b, 'aa', axis=0, tiled=True)  31.3 us
    all_gather x1, blocking collectives, per_device(): rows_a = lax.all_gather(residual_a, 'aa', axis=1, tiled=True)  30.8 us
    reduce_scatter x1, waiting for transfers between devices, per_device(): lax.psum_scatter(jnp.dot(inputs, encoder_b, preferred_element_type=jnp.fl...  30.5 us
    sub x1, other arithmetic, per_device(): correlation - 0.5 * (row_level[:, None] + column_level[None, :])  24.3 us
  transfers between devices with their start and end apart: 2, of which 1 were waited for; matrix products, arithmetic and copies ran while one was open for 1% of the time, Pallas kernels for 0%

commit v1 on v0

--- a/solution.py
+++ b/solution.py
@@ -39,7 +39,9 @@
     correlation = (
         lax.dot_general(
             every_a,
-            lax.all_gather(unit_b, "aa", axis=0, tiled=True),
+            jnp.concatenate(
+                lax.all_to_all(jnp.stack([unit_b] * lax.axis_size("aa")), "aa", 0, 0), axis=0
+            ),
             (((0,), (0,)), ((), ())),
             preferred_element_type=jnp.float32,
         )

time: 376 us -> 353 us (0.939)
  blocking collectives: 246 us -> 219 us
    all_gather x1 -> x0, blocking collectives: 31.3 us -> none  [per_device(): lax.all_gather(unit_b, 'aa', axis=0, tiled=True)]
    pmax x1, blocking collectives: 33 us -> 37.5 us  [per_device(): column_top = lax.pmax(column_local, 'aa')]
  transfers between devices with their start and end apart: 2 -> 3, of which waited for: 1 -> 1; matrix products, arithmetic and copies ran while one was open for 1% -> 3% of each run, Pallas kernels for 0% -> 0%
where the time goes in v1:
time: 353 us
  blocking collectives  219 us (62%)
  other arithmetic  56.1 us (16%)
  waiting for transfers between devices  31.1 us (9%)
  matrix products  25.9 us (7%)
  between operations  15.6 us (4%)
  starting transfers between devices  3.58 us (1%)
    pmax x1, blocking collectives, per_device(): column_top = lax.pmax(column_local, 'aa')  37.5 us
    psum x1, blocking collectives, per_device(): mean_b = lax.psum(jnp.sum(fired_b, 0), 'aa') / token_total  35 us
    psum x1, blocking collectives, per_device(): spread_b = lax.psum(jnp.sum(centered_b * centered_b, 0), 'aa') / token_total  33 us
    psum x1, blocking collectives, per_device(): lax.psum(jnp.sum(jnp.exp(scores - column_top[None, :]), axis=0), 'aa')  33 us
    all_gather x1, blocking collectives, per_device(): rows_a = lax.all_gather(residual_a, 'aa', axis=1, tiled=True)  30.8 us
    reduce_scatter x1, waiting for transfers between devices, per_device(): lax.psum_scatter(jnp.dot(inputs, encoder_b, preferred_element_type=jnp.fl...  30.5 us
    sub x1, other arithmetic, per_device(): correlation - 0.5 * (row_level[:, None] + column_level[None, :])  24.3 us
    reduce_sum x1, other arithmetic, per_device(): jnp.sum(jnp.exp(scores - row_top[:, None]), axis=1)  15.1 us
  transfers between devices with their start and end apart: 3, of which 1 were waited for; matrix products, arithmetic and copies ran while one was open for 3% of the time, Pallas kernels for 0%

profile of v1, /device:TPU:0, one launch (start us, length us, event | category | flops | bytes accessed | tf_op | source)
XLA Modules:
  0.0 352.6 jit_solution(16537722093834766318)
XLA Ops:
  8.0 0.0 reduce-scatter.2.cloned.1.call-start
  8.0 6.5 %all-gather = bf16[4,2,3584]{2,1,0:T(2,128)(2,1)S(1)} all-gather(bf16[1,2,3584]{2,1,0:T(2,128)(2,1)} %bitcast.15), channel_id=1, replica_groups=mesh['aa'=8,'ba'=4] {'ba'}, dimensions={0}, use_global_device_ids=true | all-gather | bytes 71680 | tf_op jit(solution)/shard_map/all_gather | solution.py:19
  14.5 0.1 all_to_all.17
  14.7 12.9 %all_to_all.24 = bf16[8,8,448]{2,0,1:T(8,128)(2,1)S(1)} all-to-all(bf16[8,8,448]{2,0,1:T(8,128)(2,1)S(1)} %copy.10), channel_id=1, replica_groups=mesh['aa'=8,'ba'=4] {'aa'}, dimensions={1} | all-to-all | bytes 114688 | tf_op jit(solution)/shard_map/all_to_all | solution.py:20
  27.6 3.8 %fusion.4 = f32[64,4096]{1,0:T(8,128)} fusion(bf16[448,4096]{1,0:T(8,128)(2,1)} %param.10, bf16[8,8,448]{2,0,1:T(8,128)(2,1)S(1)} %all_to_all.24), kind=kOutput, calls=%fused_computation.15 | convolution fusion | flops 234881024 | bytes 4775936 | tf_op jit(solution)/shard_map/dot_general | solution.py:23
  31.4 0.0 reduce-scatter.2.cloned.1.call-update
  31.4 0.0 all-gather.3.cloned.1.call-start
  31.5 0.5 all-gather.3.cloned.1.call-update
  32.0 30.8 %all_gather.12 = bf16[16,4096]{1,0:T(8,128)(2,1)S(1)} all-gather(bf16[16,512]{1,0:T(8,128)(2,1)} %param.6), channel_id=1, replica_groups=mesh['aa'=8,'ba'=4] {'aa'}, dimensions={1}, use_global_device_ids=true | all-gather | bytes 147456 | tf_op jit(solution)/shard_map/all_gather | solution.py:11
  62.8 30.5 %reduce-scatter.2.cloned.1.call-done = f32[8,4096]{1,0:T(8,128)} async-done(((f32[64,4096]{1,0:T(8,128)}), f32[8,4096]{1,0:T(8,128)}) %reduce-scatter.2.cloned.1.call-update) | async-done | bytes 131088 | tf_op jit(solution)/shard_map/reduce_scatter | solution.py:22
  93.3 1.0 fusion.3
  94.3 35.0 %psum.44 = f32[4096]{0:T(1024)S(1)} all-reduce(f32[4096]{0:T(1024)S(1)} %fusion.3), channel_id=1, replica_groups=mesh['aa'=8,'ba'=4] {'aa'}, use_global_device_ids=true, to_apply=%region_6.0 | all-reduce | flops 4096 | bytes 32768 | tf_op jit(solution)/shard_map/psum | solution.py:31
  129.3 1.0 multiply_reduce_fusion.2
  130.3 33.0 %psum.45 = f32[4096]{0:T(1024)S(1)} all-reduce(f32[4096]{0:T(1024)S(1)} %multiply_reduce_fusion.2), channel_id=1, replica_groups=mesh['aa'=8,'ba'=4] {'aa'}, use_global_device_ids=true, to_apply=%region_8.0 | all-reduce | flops 4096 | bytes 32768 | tf_op jit(solution)/shard_map/psum | solution.py:35
  163.3 0.9 multiply_convert_fusion
  164.2 0.8 stack.2
  165.1 3.5 all-to-all-start.1
  168.6 0.0 all-gather.3.cloned.1.call-done
  168.6 8.1 %fusion.6 = (f32[2048]{0:T(1024)S(1)}, f32[16,2048]{1,0:T(8,128)S(1)}) fusion(f32[2048]{0:T(1024)} %param.9, bf16[16,4096]{1,0:T(8,128)(2,1)S(1)} %all_gather.12, bf16[4096,2048]{1,0:T(8,128)(2,1)} %all-gather.3.cloned.1.call-done), kind=kOutput, calls=%fused_computation.23 | convolution fusion | flops 268531712 | bytes 17055744 | tf_op jit(solution)/shard_map/dot_general | solution.py:13
  176.7 5.8 %psum.42 = f32[2048]{0:T(1024)S(1)} all-reduce(f32[2048]{0:T(1024)S(1)} %get-tuple-element.5), channel_id=1, replica_groups=mesh['aa'=8,'ba'=4] {'ba'}, use_global_device_ids=true, to_apply=%region_1.0 | all-reduce | flops 2048 | bytes 16384 | tf_op jit(solution)/shard_map/psum | solution.py:30
  182.5 6.7 %psum.43 = f32[2048]{0:T(1024)S(1)} all-reduce(f32[2048]{0:T(1024)S(1)} %multiply_reduce_fusion.3), channel_id=1, replica_groups=mesh['aa'=8,'ba'=4] {'ba'}, use_global_device_ids=true, to_apply=%region_3.0 | all-reduce | flops 2048 | bytes 16384 | tf_op jit(solution)/shard_map/psum | solution.py:34
  189.2 5.8 %all_gather.14 = bf16[64,2048]{1,0:T(8,128)(2,1)S(1)} all-gather(bf16[16,2048]{1,0:T(8,128)(2,1)S(1)} %multiply_convert_fusion.1), channel_id=1, replica_groups=mesh['aa'=8,'ba'=4] {'ba'}, dimensions={0}, use_global_device_ids=true | all-gather | bytes 327680 | tf_op jit(solution)/shard_map/all_gather | solution.py:38
  195.0 0.0 all-to-all-done.1
  195.0 14.1 %multiply_reduce_fusion.1 = (f32[2048]{0:T(1024)S(1)}, f32[2048,4096]{1,0:T(8,128)}) fusion(bf16[64,2048]{1,0:T(8,128)(2,1)S(1)} %all_gather.14, bf16[8,8,4096]{2,1,0:T(8,128)(2,1)S(1)} %all-to-all-done.1), kind=kOutput, calls=%fused_computation.4 | convolution fusion | flops 1090516992 | bytes 34349056 | tf_op jit(solution)/shard_map/dot_general | solution.py:40
  209.0 6.7 %pmax.14 = f32[2048]{0:T(1024)S(1)} all-reduce(f32[2048]{0:T(1024)S(1)} %get-tuple-element.7), channel_id=1, replica_groups=mesh['aa'=8,'ba'=4] {'ba'}, use_global_device_ids=true, to_apply=%region_10.0 | all-reduce | flops 2048 | bytes 16384 | tf_op jit(solution)/shard_map/pmax | solution.py:53
  215.7 15.1 %exponential_reduce_fusion.1 = (f32[2048]{0:T(1024)S(1)}, f32[4096]{0:T(1024)S(1)}) fusion(f32[2048,4096]{1,0:T(8,128)} %get-tuple-element.8, f32[2048]{0:T(1024)S(1)} %pmax.14), kind=kLoop, calls=%fused_computation.2 | loop fusion | flops 33548288 | bytes 33587200 | tf_op jit(solution)/shard_map/reduce_sum | solution.py:55
  230.9 5.8 %psum.46 = f32[2048]{0:T(1024)S(1)} all-reduce(f32[2048]{0:T(1024)S(1)} %get-tuple-element.3), channel_id=1, replica_groups=mesh['aa'=8,'ba'=4] {'ba'}, use_global_device_ids=true, to_apply=%region_12.0 | all-reduce | flops 2048 | bytes 16384 | tf_op jit(solution)/shard_map/psum | solution.py:55
  236.7 0.0 copy-start.1
  236.7 37.5 %pmax.15 = f32[4096]{0:T(1024)S(1)} all-reduce(f32[4096]{0:T(1024)S(1)} %get-tuple-element.4), channel_id=1, replica_groups=mesh['aa'=8,'ba'=4] {'aa'}, use_global_device_ids=true, to_apply=%region_14.0 | all-reduce | flops 4096 | bytes 32768 | tf_op jit(solution)/shard_map/pmax | solution.py:54
  274.1 13.7 %exponential_reduce_fusion = f32[4096]{0:T(1024)S(1)} fusion(f32[2048,4096]{1,0:T(8,128)} %get-tuple-element.8, f32[4096]{0:T(1024)S(1)} %pmax.15), kind=kLoop, calls=%fused_computation.1 | loop fusion | flops 25161728 | bytes 33587200 | tf_op jit(solution)/shard_map/reduce_sum | solution.py:56
  287.9 33.0 %psum.47 = f32[4096]{0:T(1024)S(1)} all-reduce(f32[4096]{0:T(1024)S(1)} %exponential_reduce_fusion), channel_id=1, replica_groups=mesh['aa'=8,'ba'=4] {'aa'}, use_global_device_ids=true, to_apply=%region_16.0 | all-reduce | flops 4096 | bytes 32768 | tf_op jit(solution)/shard_map/psum | solution.py:56
  320.9 0.0 copy-start
  320.9 24.3 %multiply_subtract_fusion = f32[2048,4096]{1,0:T(8,128)} fusion(f32[2048,4096]{1,0:T(8,128)} %get-tuple-element.8, f32[4096]{0:T(1024)S(1)} %add_multiply_fusion, f32[2048]{0:T(1024)S(1)} %add_multiply_fusion.1), kind=kLoop, calls=%fused_computation | loop fusion | flops 33554432 | bytes 67133440 | tf_op jit(solution)/shard_map/sub | solution.py:59
  345.1 0.0 copy-done.1
  345.1 0.0 copy-done
  (9 shorter events, 0.1 us)
Async XLA Ops:
  8.0 85.3 %reduce-scatter.2.cloned.1.call-start = ((), (), s32[]{:S(2)}) async-start(), calls=%async_computation.4 | async-start | bytes 1179648 | tf_op jit(solution)/shard_map/reduce_scatter | solution.py:22
  31.4 137.2 %all-gather.3.cloned.1.call-start = ((), (), s32[]{:S(2)}) async-start(), calls=%async_computation.3 | async-start | bytes 20971520 | tf_op jit(solution)/shard_map/all_gather | solution.py:15
  165.1 29.9 %all-to-all-start.1 = ((bf16[8,8,4096]{2,1,0:T(8,128)(2,1)}), bf16[8,8,4096]{2,1,0:T(8,128)(2,1)S(1)}, u32[]{:S(2)}, u32[]{:S(2)}) async-start(bf16[8,8,4096]{2,1,0:T(8,128)(2,1)} %stack.2), calls=%async_computation.2 | async-start | bytes 1048576 | tf_op jit(solution)/shard_map/all_to_all | solution.py:43
  236.7 108.5 %copy-start.1 = (f32[2048]{0:T(1024)}, f32[2048]{0:T(1024)S(1)}, u32[]{:S(2)}) copy-start(f32[2048]{0:T(1024)S(1)} %add_multiply_fusion.1) | copy-start | bytes 24580
  320.9 24.3 %copy-start = (f32[4096]{0:T(1024)}, f32[4096]{0:T(1024)S(1)}, u32[]{:S(2)}) copy-start(f32[4096]{0:T(1024)S(1)} %add_multiply_fusion) | copy-start | bytes 49156
Sparse Core Ops, SparseCore 0:
  31.5 61.7 reduce-scatter.1
Sparse Core Ops, SparseCore 1:
  33.5 103.3 all-gather.2
